TPU v7x, 32 devices: a whole 2x2x4 slice. The times are simulated.
32 devices in a mesh: gx: 4 (over y, x), gy: 2 (over core), gz: 4 (over z).
Axes of the slice: x: 2, y: 2, z: 4, core: 2. Of those that a mesh axis runs over, the one named last changes fastest.
Arguments:
- residual_in: float32 [256, 128, 1024], P('gx', 'gy', 'gz'), may hold values from -700 to 700
Outputs:
- level_one: float32 [128, 64, 512], P('gx', 'gy', 'gz')
- level_two: float32 [64, 32, 256], P('gx', 'gy', 'gz')
- level_three: float32 [32, 16, 128], P('gx', 'gy', 'gz')
- level_four: float32 [16, 8, 64], P('gx', 'gy', 'gz')
- level_five: float32 [8, 4, 32], P('gx', 'gy', 'gz')
- level_scales: float32 [5], replicated
All inputs are finite; a program needn't handle non-finite values.
Results may differ from a plain program's by a relative error of at most 0.0002.
Values sent between devices are 32-bit elements; how exact they have to be, the bound alone decides.
A program may use at most 64 MiB of HBM per device.

v0:
```python
import functools

import jax
import jax.numpy as jnp
import ml_dtypes
import numpy as np
from jax import lax
from jax.experimental import pallas as pl
from jax.experimental.pallas import tpu as pltpu
from jax.sharding import PartitionSpec as P

LEVELS = 5
EPSILON = 1e-06
LANES = 128
AXES = ("gx", "gy", "gz")
MESH = pl.DeviceIdType.MESH
HOPS = ((1, 0, 0), (0, 1, 0), (1, 1, 0), (0, 0, 1), (1, 0, 1), (0, 1, 1), (1, 1, 1))


def round_up(n, m):
    return -(-n // m) * m


def step_matrix(n_in, n_cells):
    out = np.zeros((n_cells // 2 + 1, n_in))
    for i in range(n_cells // 2 + 1):
        for off, w in ((-1, 0.25), (0, 0.5), (1, 0.25)):
            if 0 <= 2 * i + off < n_in:
                out[i, 2 * i + off] = w
    return out


def composites(cells):
    mats, m, n = [], None, cells // 2
    for _ in range(LEVELS - 1):
        s = step_matrix(n + 1, n)
        m = s if m is None else s @ m
        mats.append(m)
        n //= 2
    return mats


def exact(table):
    out = table.astype(np.float32).astype(ml_dtypes.bfloat16)
    assert (out.astype(np.float64) == table).all()
    return out


class Plan:
    def __init__(self, shape):
        self.nx, self.ny, self.nz = shape
        self.x1, self.y1, self.z1 = (n // 2 for n in shape)
        assert self.z1 == LANES and self.y1 % 8 == 0
        self.xs = [self.nx >> l for l in range(2, LEVELS + 1)]
        self.ys = [self.ny >> l for l in range(2, LEVELS + 1)]
        self.zs = [self.nz >> l for l in range(2, LEVELS + 1)]
        self.pys = [round_up(y, 8) for y in self.ys]
        self.pxs = [round_up(x, 8) for x in self.xs]
        self.base = np.concatenate([[0], np.cumsum([x * p for x, p in zip(self.xs, self.pys)])]).tolist()
        self.own = round_up(self.base[-1], LANES)
        self.xoff = np.concatenate([[0], np.cumsum(self.pys)]).tolist()
        self.yoff = np.concatenate([[0], np.cumsum(self.pxs)]).tolist()
        self.bx = max(self.y1, self.xoff[-1])
        self.by = max(self.x1, self.yoff[-1])
        self.y0 = self.bx
        self.c0 = self.bx + self.by
        assert self.c0 + 8 <= LANES and self.x1 <= LANES
        self.coff = np.concatenate([[0], np.cumsum(self.zs)]).tolist()
        assert self.coff[-1] <= LANES
        self.main = self.x1 * self.y1
        self.rows1 = self.main + LANES
        self.crows = self.own + LANES

    def row1(self, i, j):
        if i < self.x1 and j < self.y1:
            return i * self.y1 + j
        if j < self.y1:
            return self.main + j
        if i < self.x1:
            return self.main + self.y0 + i
        return self.main + self.c0

    def tables(self):
        xm, ym, zm = composites(self.nx), composites(self.ny), composites(self.nz)
        order = np.array([[self.row1(i, j) for j in range(self.y1 + 1)] for i in range(self.x1 + 1)])
        big = np.zeros((self.crows, self.rows1))
        spread = np.zeros((self.own, LANES))
        for l in range(LEVELS - 1):
            nx, ny = self.xs[l], self.ys[l]
            for i in range(nx + 1):
                for j in range(ny + 1):
                    if i < nx and j < ny:
                        r = self.base[l] + i * self.pys[l] + j
                    elif j < ny:
                        r = self.own + self.xoff[l] + j
                    elif i < nx:
                        r = self.own + self.y0 + self.yoff[l] + i
                    else:
                        r = self.own + self.c0 + l
                    big[r, order] = xm[l][i][:, None] * ym[l][j][None, :]
            for j in range(ny):
                spread[self.base[l] + j, self.xoff[l] + j] = 1
            for i in range(nx):
                spread[self.base[l] + i * self.pys[l], self.y0 + self.yoff[l] + i] = 1
            spread[self.base[l], self.c0 + l] = 1
        z_first = step_matrix(self.nz, self.nz)
        kz1 = np.zeros((self.nz, 2 * LANES))
        kz1[:, :LANES] = z_first[:LANES].T
        kz1[:, LANES:] = z_first[LANES][:, None]
        kz = np.zeros((2 * LANES, LANES))
        tails = np.zeros((16, 2 * LANES))
        place = np.zeros((16, 2 * LANES))
        for l in range(LEVELS - 1):
            kz[: LANES + 1, self.coff[l] : self.coff[l + 1]] = zm[l][:-1].T
            tails[l, : LANES + 1] = zm[l][-1]
            place[l, LANES + self.coff[l]] = 1
        tail1 = np.zeros((16, self.nz))
        tail1[LEVELS - 1] = z_first[LANES]
        place[LEVELS - 1, 0] = 1
        return self.pack([kz1, kz, tails, tail1, place, spread], big)

    def pack(self, small, big):
        blocks = -(-self.rows1 // self.nz)
        rows = [np.zeros((self.crows, self.nz)) for _ in range(blocks)]
        for n, block in enumerate(rows):
            part = big[:, n * self.nz : (n + 1) * self.nz]
            block[:, : part.shape[1]] = part
        self.places, self.small = [], []
        at = blocks * self.crows
        for t in small:
            block = np.zeros((t.shape[0], self.nz))
            block[:, : t.shape[1]] = t
            rows.append(block)
            self.places.append((at, 0))
            self.small.append(t.shape)
            at += t.shape[0]
        return exact(np.concatenate(rows))


def halves(x):
    hi = x.astype(jnp.bfloat16)
    return hi, (x - hi.astype(jnp.float32)).astype(jnp.bfloat16)


def dot(a, b, dims=((1,), (0,))):
    return lax.dot_general(a, b, (dims, ((), ())), preferred_element_type=jnp.float32)


def gather_kernel(plan, sizes, chunks, *refs):
    p = plan
    v_hbm, packed_hbm = refs[:2]
    out1_hbm, outc_hbm, stats = refs[2:5]
    (vin, planes, spill, uhi, ulo, z, zhi, zlo, dacc) = refs[5:14]
    tabs = refs[14:21]
    sends = refs[21:30]
    recvs = refs[30:39]
    mine, parts = refs[39:41]
    vsem, tsem, bsem, ssem, rsem, asend, arecv = refs[41:48]
    out1, outc, osem = refs[48:51]
    kz1, kz, tails, tail1, place, spread, big = tabs
    pos = [lax.axis_index(a) for a in AXES]
    group = sizes[0] * sizes[1]
    me = pos[0] * sizes[1] + pos[1]

    in_plane = []
    for k in range(group):
        r = lax.rem(me + k, group)
        in_plane.append((r // sizes[1], lax.rem(r, sizes[1])))
    in_line = [lax.rem(pos[2] + k, sizes[2]) for k in range(sizes[2])]
    others = [
        {"gx": gx, "gy": gy, "gz": gz} for gz in in_line for gx, gy in in_plane
    ][1:]

    def along(hop, way):
        ok, target = None, {}
        for a in range(3):
            target[AXES[a]] = pos[a]
            if hop[a]:
                here = pos[a] < sizes[a] - 1 if way > 0 else pos[a] > 0
                ok = here if ok is None else jnp.logical_and(ok, here)
                target[AXES[a]] = lax.rem(pos[a] + way + sizes[a], sizes[a])
        return ok, target

    per = p.nx // chunks
    tcopies = [
        pltpu.make_async_copy(
            packed_hbm.at[pl.ds(at, t.shape[0]), pl.ds(lane, t.shape[1])], t, tsem.at[n]
        )
        for n, (t, (at, lane)) in enumerate(zip(tabs[:6], p.places))
    ]
    blocks = -(-p.rows1 // p.nz)
    bcopies = []
    for n in range(blocks):
        width = min(p.nz, p.rows1 - n * p.nz)
        bcopies.append(
            pltpu.make_async_copy(
                packed_hbm.at[pl.ds(n * p.crows, p.crows), pl.ds(0, width)],
                big.at[:, pl.ds(n * p.nz, width)],
                bsem.at[n],
            )
        )
    vcopies = [
        pltpu.make_async_copy(
            v_hbm.at[pl.ds(c * per, per)], vin.at[pl.ds(1 + c * per, per)], vsem.at[c]
        )
        for c in range(chunks)
    ]
    vcopies[0].start()
    for c in tcopies + vcopies[1:] + bcopies:
        c.start()

    barrier = pltpu.get_barrier_semaphore()
    for target in others:
        pl.semaphore_signal(barrier, inc=1, device_id=target, device_id_type=MESH)

    half = per // 2
    vin[0] = jnp.zeros((p.ny, p.nz), jnp.float32)
    lanes = lax.broadcasted_iota(jnp.int32, (p.y1, LANES), 1)
    spill[...] = jnp.zeros_like(spill)
    for j in range(half):
        planes[j, :, 0:8, :] = jnp.zeros((2, 8, LANES), jnp.float32)
    dacc[...] = jnp.zeros_like(dacc)
    for i in range(6):
        tcopies[i].wait()

    def fold_y(j):
        cols = []
        for h in range(2):
            even = planes[j, h, pl.ds(8, p.y1, 2), :]
            odd = planes[j, h, pl.ds(9, p.y1, 2), :]
            prev = planes[j, h, pl.ds(7, p.y1, 2), :]
            cols.append(0.5 * even + 0.25 * (odd + prev))
        return jnp.concatenate(cols, axis=1)

    def last_y(j):
        end = 8 + p.ny
        return jnp.concatenate(
            [0.25 * planes[j, h, end - 1 : end, :] for h in range(2)], axis=1
        )

    def put_plane(j, t):
        for h in range(2):
            planes[j, h, 8:, :] = t[:, h * LANES : (h + 1) * LANES]

    for c in range(chunks):
        vcopies[c].wait()

        @pl.loop(0, half)
        def _(j):
            i = c * half + j
            put_plane(j, 0.5 * vin[2 * i + 1] + 0.25 * (vin[2 * i + 2] + vin[2 * i]))
            hi, lo = halves(fold_y(j))
            rows = pl.ds(pl.multiple_of(i * p.y1, p.y1), p.y1)
            uhi[rows, :] = hi
            ulo[rows, :] = lo
            spill[pl.ds(p.y0 + i, 1), :] = last_y(j)

        rows = pl.ds(c * half * p.y1, half * p.y1)
        z[rows, :] = dot(uhi[rows, :], kz1[...]) + dot(ulo[rows, :], kz1[...])

        @pl.loop(0, half)
        def _(j):
            i = c * half + j
            rows = pl.ds(pl.multiple_of(i * p.y1, p.y1), p.y1)
            plane = z[rows, :]
            dacc[...] += jnp.where(lanes == i, plane[:, LANES:], 0.0)
            hi, lo = halves(plane)
            zhi[rows, :] = hi
            zlo[rows, :] = lo

    put_plane(0, 0.25 * vin[p.nx])
    spill[0 : p.y1, :] = fold_y(0)
    spill[p.c0 : p.c0 + 1, :] = last_y(0)
    shi, slo = halves(spill[...])
    zs = dot(shi, kz1[...]) + dot(slo, kz1[...])
    hi, lo = halves(zs)
    zhi[p.main :, :] = hi
    zlo[p.main :, :] = lo
    tail_one = dot(tail1[...], shi, ((1,), (1,))) + dot(tail1[...], slo, ((1,), (1,)))
    mx1, my1, mxy1, mz1, mxc, myc, mxyc, mzc, m8 = sends
    mx1[...] = zs[0 : p.bx, :LANES]
    my1[...] = zs[p.y0 : p.c0, :LANES]
    mxy1[...] = zs[p.c0 : p.c0 + 8, :LANES]
    mz1[...] = dacc[...]
    pl.semaphore_wait(barrier, len(others))

    rx1, ry1, rxy1, rz1, rxc, ryc, rxyc, rzc, r8 = recvs
    srcs = [mx1, my1, mxy1, mz1, mxc, myc, mxyc, mzc, m8, m8, m8]
    dsts = [rx1, ry1, rxy1, rz1, rxc, ryc, rxyc, rzc, r8.at[0], r8.at[1], r8.at[2]]
    hops = HOPS[:4] + HOPS[:4] + HOPS[4:]
    has_next, has_prev, copies = [], [], []
    for n, hop in enumerate(hops):
        ok_n, target = along(hop, 1)
        has_next.append(ok_n)
        has_prev.append(along(hop, -1)[0])
        copies.append(
            pltpu.make_async_remote_copy(
                src_ref=srcs[n],
                dst_ref=dsts[n],
                send_sem=ssem.at[n],
                recv_sem=rsem.at[n],
                device_id=target,
                device_id_type=MESH,
            )
        )

    def send(which):
        for n in which:

            @pl.when(has_next[n])
            def _():
                copies[n].start()

    send((0, 3, 1, 2))
    for n in range(len(hops)):

        @pl.when(jnp.logical_not(has_prev[n]))
        def _():
            dsts[n][...] = jnp.zeros(dsts[n].shape, jnp.float32)

    for c in bcopies:
        c.wait()
    b = dot(big[...], zhi[...]) + dot(big[...], zlo[...])
    bhi, blo = halves(b)
    cs = dot(bhi, kz[...]) + dot(blo, kz[...])
    tail_c = dot(tails[...], bhi, ((1,), (1,))) + dot(tails[...], blo, ((1,), (1,)))

    mxc[...] = cs[p.own : p.own + p.bx]
    myc[...] = cs[p.own + p.y0 : p.own + p.c0]
    mxyc[...] = cs[p.own + p.c0 : p.own + p.c0 + 8]
    groups = p.own // LANES
    for g in range(groups):
        mzc[8 * g : 8 * g + 8, :] = tail_c[0:8, g * LANES : (g + 1) * LANES]
    m8[...] = tail_one[0:8] + tail_c[0:8, p.own :]
    send((10, 8, 4, 7, 9, 5, 6))

    for n in range(len(hops)):

        @pl.when(has_prev[n])
        def _():
            copies[n].wait_recv()

    lane8 = lax.broadcasted_iota(jnp.int32, (8, LANES), 1)
    g8 = jnp.where(lane8 < p.y0, r8[0], jnp.where(lane8 < p.c0, r8[1], r8[2]))

    def turned(x, where):
        hi, lo = halves(x.T)
        return dot(hi, where) + dot(lo, where)

    f = turned(g8, place[0:8, :])
    xs1 = rx1[...] + f[0 : p.bx, :LANES]
    ys1 = ry1[...] + f[p.y0 : p.c0, :LANES]
    xy1 = rxy1[...] + f[p.c0 : p.c0 + 8, :LANES]
    pieces = [
        rxc[...] + f[0 : p.bx, LANES:],
        ryc[...] + f[p.y0 : p.c0, LANES:],
        rxyc[...] + f[p.c0 : p.c0 + 8, LANES:],
    ]
    if p.c0 + 8 < LANES:
        pieces.append(jnp.zeros((LANES - p.c0 - 8, LANES), jnp.float32))
    whi, wlo = halves(jnp.concatenate(pieces, axis=0))
    c = cs[0 : p.own] + dot(spread[...], whi) + dot(spread[...], wlo)
    c = c + jnp.concatenate(
        [
            turned(rzc[8 * g : 8 * g + 8, :], place[0:8, LANES:])
            for g in range(groups)
        ],
        axis=0,
    )
    outc[...] = c

    first = lanes == 0
    top = lax.broadcasted_iota(jnp.int32, (p.y1, LANES), 0) == 0
    col = rz1[...]
    acc = jnp.zeros((p.y1, LANES), jnp.float32)
    for i in range(p.x1):
        shifted = pltpu.roll(col, (LANES - i) % LANES, 1) if i else col
        plane = z[i * p.y1 : (i + 1) * p.y1, :LANES] + jnp.where(first, shifted, 0.0)
        edge = ys1[i : i + 1, :]
        if i == 0:
            plane = plane + xs1[0 : p.y1]
            edge = edge + xy1[0:1, :]
        plane = plane + jnp.where(top, edge, 0.0)
        out1[i] = plane
        acc = acc + plane * plane
    results = [
        pltpu.make_async_copy(out1, out1_hbm, osem.at[0]),
        pltpu.make_async_copy(outc, outc_hbm, osem.at[1]),
    ]
    mine[0:1, :] = jnp.sum(acc, axis=0, keepdims=True)
    sq = c * c
    lane1 = lax.broadcasted_iota(jnp.int32, (1, LANES), 1)
    row = jnp.zeros((1, LANES), jnp.float32)
    for l in range(LEVELS - 1):
        total = jnp.sum(sq[p.base[l] : p.base[l + 1]], axis=0, keepdims=True)
        row = jnp.where((lane1 >= p.coff[l]) & (lane1 < p.coff[l + 1]), total, row)
    mine[1:2, :] = row

    for c in results:
        c.start()

    pending = [
        pltpu.make_async_remote_copy(
            src_ref=mine,
            dst_ref=parts.at[k + 1],
            send_sem=asend.at[k],
            recv_sem=arecv.at[k],
            device_id=target,
            device_id_type=MESH,
        )
        for k, target in enumerate(others)
    ]
    for c in reversed(pending):
        c.start()
    parts[0] = mine[...]
    for c in pending:
        c.wait_recv()
    stats[...] = jnp.sum(parts[...], axis=0)
    for c in results:
        c.wait()
    for c in pending:
        c.wait_send()
    for n in range(len(hops)):

        @pl.when(has_next[n])
        def _():
            copies[n].wait_send()


def scale_kernel(plan, devices, grid, packed, stats, o1, o2, o3, o4, o5, scales):
    p = plan
    lane1 = lax.broadcasted_iota(jnp.int32, (1, LANES), 1)
    outs = (o1, o2, o3, o4, o5)
    product = jnp.ones((1, 1), jnp.float32)
    for l in range(LEVELS):
        row = stats[0:1, :] if l == 0 else stats[1:2, :]
        if l:
            row = jnp.where(
                (lane1 >= p.coff[l - 1]) & (lane1 < p.coff[l]), row, 0.0
            )
        total = jnp.sum(row, axis=1, keepdims=True)
        cells = devices * (p.nx >> (l + 1)) * (p.ny >> (l + 1)) * (p.nz >> (l + 1))
        scale = jnp.sqrt(total / (product * product) / cells + EPSILON)
        product = product * scale
        scales[l] = scale[0, 0]
        inverse = 1.0 / product
        if l == 0:
            o1[...] = grid[...] * inverse.reshape(1, 1, 1)
            continue
        k = l - 1
        block = packed[p.base[k] : p.base[k + 1], :] * inverse
        if p.coff[k]:
            block = pltpu.roll(block, LANES - p.coff[k], 1)
        block = block.reshape(p.xs[k], p.pys[k], LANES)
        outs[l][...] = block[:, : p.ys[k], : p.zs[k]]


def per_device(sizes, residual_in):
    plan = Plan(residual_in.shape)
    p = plan
    packed_table = p.tables()
    chunks = 4
    count = sizes[0] * sizes[1] * sizes[2]
    f32, bf16 = jnp.float32, jnp.bfloat16
    ends = [(p.bx, LANES), (p.by, LANES), (8, LANES)]
    messages = ends + [(p.y1, LANES)] + ends + [(8 * (p.own // LANES), LANES)]
    anywhere = pl.BlockSpec(memory_space=pl.ANY)
    vmem = pl.BlockSpec(memory_space=pltpu.VMEM)
    dma = pltpu.SemaphoreType.DMA
    grid, packed, stats = pl.pallas_call(
        functools.partial(gather_kernel, p, sizes, chunks),
        out_shape=(
            jax.ShapeDtypeStruct((p.x1, p.y1, p.z1), f32),
            jax.ShapeDtypeStruct((p.own, LANES), f32),
            jax.ShapeDtypeStruct((2, LANES), f32),
        ),
        in_specs=[anywhere] * 2,
        out_specs=(anywhere, anywhere, vmem),
        scratch_shapes=[
            pltpu.VMEM((p.nx + 1, p.ny, p.nz), f32),
            pltpu.VMEM((p.nx // chunks // 2, 2, 8 + p.ny, LANES), f32),
            pltpu.VMEM((LANES, p.nz), f32),
            pltpu.VMEM((p.main, p.nz), bf16),
            pltpu.VMEM((p.main, p.nz), bf16),
            pltpu.VMEM((p.main, 2 * LANES), f32),
            pltpu.VMEM((p.rows1, 2 * LANES), bf16),
            pltpu.VMEM((p.rows1, 2 * LANES), bf16),
            pltpu.VMEM((p.y1, LANES), f32),
        ]
        + [pltpu.VMEM(t, bf16) for t in p.small + [(p.crows, p.rows1)]]
        + [pltpu.VMEM(s, f32) for s in messages + [(8, LANES)]]
        + [pltpu.VMEM(s, f32) for s in messages + [(3, 8, LANES)]]
        + [
            pltpu.VMEM((2, LANES), f32),
            pltpu.VMEM((count, 2, LANES), f32),
            dma((chunks,)),
            dma((6,)),
            dma((-(-p.rows1 // p.nz),)),
            dma((11,)),
            dma((11,)),
            dma((count - 1,)),
            dma((count - 1,)),
            pltpu.VMEM((p.x1, p.y1, p.z1), f32),
            pltpu.VMEM((p.own, LANES), f32),
            dma((2,)),
        ],
        compiler_params=pltpu.CompilerParams(collective_id=0, has_side_effects=True),
        name="restrict_exchange",
    )(residual_in, jnp.asarray(packed_table))
    shapes = [
        (p.nx >> l, p.ny >> l, p.nz >> l) for l in range(1, LEVELS + 1)
    ]
    return pl.pallas_call(
        functools.partial(scale_kernel, p, count),
        out_shape=tuple(jax.ShapeDtypeStruct(s, f32) for s in shapes)
        + (jax.ShapeDtypeStruct((LEVELS,), f32),),
        in_specs=[vmem] * 3,
        out_specs=(vmem,) * 5 + (pl.BlockSpec(memory_space=pltpu.SMEM),),
        name="scale_levels",
    )(grid, packed, stats)


def solution(mesh):
    sizes = tuple(mesh.shape[a] for a in AXES)
    spec = P(*AXES)
    return jax.shard_map(
        functools.partial(per_device, sizes),
        mesh=mesh,
        in_specs=(spec,),
        out_specs=(spec,) * 5 + (P(),),
        check_vma=False,
    )
```

profile of v0, /device:TPU:0, one launch (start us, length us, event | category | flops | bytes accessed | tf_op | source)
XLA Modules:
  0.0 22.9 jit_solution(7300576393455790638)
XLA Ops:
  0.6 20.1 %restrict_exchange.1 = (f32[32,32,128]{2,1,0:T(8,128)}, f32[384,128]{1,0:T(8,128)}, f32[2,128]{1,0:T(2,128)}) custom-call(f32[64,64,256]{2,1,0:T(8,128)} %refs_0_.1, bf16[3504,256]{1,0:T(8,128)(2,1)} %constant.2.clone.refs_1_), custom_call_target="tpu_custom_call" | custom-call | tf_op jit(solution)/shard_map/restrict_exchange/pallas_call | solution.py:470
  20.7 2.1 %scale_levels.1 = (f32[32,32,128]{2,1,0:T(8,128)}, f32[16,16,64]{2,1,0:T(8,128)}, f32[8,8,32]{2,1,0:T(8,128)}, f32[4,4,16]{2,1,0:T(4,128)}, f32[2,2,8]{2,1,0:T(2,128)}, /*index=5*/f32[5]{0:T(128)}) custom-call(f32[32,32,128]{2,1,0:T(8,128)} %get-tuple-element.9.grid, f32[384,128]{1,0:T(8,128)} %get-tuple-element.10.packed, f32[2,128]{1,0:T(2,128)} %get-tuple-element.11.stats), custom_call_target="tpu_custom_call" | custom-call | tf_op jit(solution)/shard_map/scale_levels/pallas_call | solution.py:513
where the time goes:
time: 23 us; the launch traced here: 22.9 us
  Pallas kernels  22.2 us (97%)
  between operations  0.64 us (3%)
    pallas_call x1, Pallas kernels, per_device(): pl.pallas_call(functools.partial(gather_kernel, p, sizes, chunks), out_sh...  20.1 us
    pallas_call x1, Pallas kernels, per_device(): pl.pallas_call(functools.partial(scale_kernel, p, count), out_shape=tuple...  2.13 us

commit v1 on v0

v1 whole, which is shorter than its diff:
```python
import functools

import jax
import jax.numpy as jnp
import ml_dtypes
import numpy as np
from jax import lax
from jax.experimental import pallas as pl
from jax.experimental.pallas import tpu as pltpu
from jax.sharding import PartitionSpec as P

LEVELS = 5
EPSILON = 1e-06
LANES = 128
PAD = 8
CHUNKS = 4
AXES = ("gx", "gy", "gz")
MESH = pl.DeviceIdType.MESH
HOPS = ((1, 1, 1), (1, 0, 1), (0, 1, 1), (0, 0, 1), (1, 0, 0), (1, 1, 0), (0, 1, 0))


def round_up(n, m):
    return -(-n // m) * m


def step_matrix(n_in, n_cells):
    out = np.zeros((n_cells // 2 + 1, n_in))
    for i in range(n_cells // 2 + 1):
        for off, w in ((-1, 0.25), (0, 0.5), (1, 0.25)):
            if 0 <= 2 * i + off < n_in:
                out[i, 2 * i + off] = w
    return out


def exact(table):
    out = table.astype(np.float32).astype(ml_dtypes.bfloat16)
    assert (out.astype(np.float64) == table).all()
    return out


class Plan:
    def __init__(self, shape):
        self.nx, self.ny, self.nz = shape
        self.xs = [self.nx >> l for l in range(1, LEVELS + 1)]
        self.ys = [self.ny >> l for l in range(1, LEVELS + 1)]
        self.zs = [self.nz >> l for l in range(1, LEVELS + 1)]
        assert self.zs[0] == LANES and self.ys[0] % 8 == 0
        self.ext = [round_up(y + 1, 8) for y in self.ys]
        self.pys = [round_up(y, 8) for y in self.ys]
        self.coff = [0] + np.concatenate([[0], np.cumsum(self.zs[1:])]).tolist()
        self.end = self.coff[-1]
        self.tail = [self.end + LEVELS - 1] + [self.end + l for l in range(LEVELS - 1)]
        assert self.end + LEVELS <= LANES
        self.zoff = np.concatenate([[0], np.cumsum(self.xs)]).tolist()
        assert self.zoff[-1] <= LANES
        rows = [x * p for x, p in zip(self.xs[1:], self.pys[1:])]
        self.base = [0] + np.concatenate([[0], np.cumsum(rows)]).tolist()
        self.own = self.base[-1]
        self.stage = [PAD + max(self.ext[l - 1], 2 * self.ext[l]) for l in range(1, LEVELS)]

    def table(self):
        m = step_matrix(self.nz, self.nz)
        out = np.zeros((self.nz, 2 * LANES))
        out[:, :LANES] = m[:-1].T
        out[:, LANES + self.tail[0]] = m[-1]
        for l in range(1, LEVELS):
            m = step_matrix(self.zs[l - 1] + 1, self.zs[l - 1]) @ m
            at = LANES + self.coff[l]
            out[:, at : at + self.zs[l]] = m[:-1].T
            out[:, LANES + self.tail[l]] = m[-1]
        return exact(out / 16)


def halves(x):
    hi = x.astype(jnp.bfloat16)
    return hi, (x - hi.astype(jnp.float32)).astype(jnp.bfloat16)


def dot(a, b):
    return lax.dot_general(a, b, (((1,), (0,)), ((), ())), preferred_element_type=jnp.float32)


def roll(x, shift):
    shift %= LANES
    return pltpu.roll(x, shift, 1) if shift else x


def gather_kernel(plan, sizes, *refs):
    p = plan
    v_hbm, table_hbm = refs[:2]
    out1_hbm, outc_hbm, stats = refs[2:5]
    vin, table = refs[5:7]
    stages = refs[7:11]
    sends = refs[11:18]
    recvs = refs[18:25]
    mine, parts = refs[25:27]
    vsem, tsem, ssem, rsem, asend, arecv = refs[27:33]
    out1, outc, osem = refs[33:36]
    f32 = jnp.float32
    pos = [lax.axis_index(a) for a in AXES]
    group = sizes[0] * sizes[1]
    me = pos[0] * sizes[1] + pos[1]
    x1, y1 = p.xs[0], p.ys[0]

    in_plane = []
    for k in range(group):
        r = lax.rem(me + k, group)
        in_plane.append((r // sizes[1], lax.rem(r, sizes[1])))
    in_line = [lax.rem(pos[2] + k, sizes[2]) for k in range(sizes[2])]
    others = [
        {"gx": gx, "gy": gy, "gz": gz} for gz in in_line for gx, gy in in_plane
    ][1:]

    def along(hop, way):
        ok, target = None, {}
        for a in range(3):
            target[AXES[a]] = pos[a]
            if hop[a]:
                here = pos[a] < sizes[a] - 1 if way > 0 else pos[a] > 0
                ok = here if ok is None else jnp.logical_and(ok, here)
                target[AXES[a]] = lax.rem(pos[a] + way + sizes[a], sizes[a])
        return ok, target

    per = p.nx // CHUNKS
    tcopy = pltpu.make_async_copy(table_hbm, table, tsem.at[0])
    vcopies = [
        [
            pltpu.make_async_copy(
                v_hbm.at[pl.ds(c * per, per), :, pl.ds(h * LANES, LANES)],
                vin.at[pl.ds(c * per, per), h, pl.ds(PAD, p.ny)],
                vsem.at[2 * c + h],
            )
            for h in range(2)
        ]
        for c in range(CHUNKS)
    ]
    for pair in vcopies[:1]:
        for c in pair:
            c.start()
    tcopy.start()
    for pair in vcopies[1:]:
        for c in pair:
            c.start()

    barrier = pltpu.get_barrier_semaphore()
    for target in others:
        pl.semaphore_signal(barrier, inc=1, device_id=target, device_id_type=MESH)

    after = PAD + p.ny
    for x in range(p.nx):
        for h in range(2):
            vin[x, h, 0:PAD, :] = jnp.zeros((PAD, LANES), f32)
            vin[x, h, after:, :] = jnp.zeros((2 * PAD, LANES), f32)
    for l in range(1, LEVELS):
        s = stages[l - 1]
        for k in range(p.xs[l] + 1):
            s[k, 0:PAD, :] = jnp.zeros((PAD, LANES), f32)
            rest = p.stage[l - 1] - PAD - p.ext[l - 1]
            if rest:
                s[k, PAD + p.ext[l - 1] :, :] = jnp.zeros((rest, LANES), f32)

    def plane_of(x):
        cols = []
        for h in range(2):
            even = vin[x, h, pl.ds(PAD, y1, 2), :]
            odd = vin[x, h, pl.ds(PAD + 1, y1, 2), :]
            prev = vin[x, h, pl.ds(PAD - 1, y1, 2), :]
            last = vin[x, h, pl.ds(after - 1, 8, 2), :]
            cols.append(jnp.concatenate([(even + even) + (odd + prev), last], axis=0))
        return jnp.concatenate(cols, axis=1)

    def lanes_of(n):
        return lax.broadcasted_iota(jnp.int32, (n, LANES), 1)

    def fold_x(planes, k, n):
        if k == n:
            return 0.25 * planes[2 * k - 1] + 0.5 * planes[2 * k]
        sides = planes[2 * k + 1] + planes[2 * k - 1] if k else planes[1]
        return 0.5 * planes[2 * k] + 0.25 * sides

    def fold_y(s, k, n):
        even = s[k, pl.ds(PAD, n, 2), :]
        odd = s[k, pl.ds(PAD + 1, n, 2), :]
        prev = s[k, pl.ds(PAD - 1, n, 2), :]
        return 0.5 * even + 0.25 * (odd + prev)

    xyz, zx, yz, zf, xf, xy, yf = sends
    half = per // 2
    rows = p.ext[0]
    lane = lanes_of(rows)
    comps = []
    columns = [jnp.zeros((e, LANES), f32) for e in p.ext]
    before = None
    tcopy.wait()
    for c in range(CHUNKS):
        for copy in vcopies[c]:
            copy.wait()
        us = []
        for j in range(half):
            i = c * half + j
            even, odd = plane_of(2 * i), plane_of(2 * i + 1)
            t = (even + even) + odd
            us.append(t if before is None else t + before)
            before = odd
        if c == CHUNKS - 1:
            us.append(before)
        count = len(us)
        if count * rows % 16:
            us.append(jnp.zeros((8, p.nz), f32))
        hi, lo = halves(jnp.concatenate(us, axis=0))
        z = dot(hi, table[...]) + dot(lo, table[...])
        for j in range(count):
            i = c * half + j
            plane = z[j * rows : (j + 1) * rows]
            comp = plane[:, LANES:]
            comps.append(comp)
            moved = roll(comp, (i % x1) - p.tail[0])
            if i < x1:
                out1[i] = plane[:y1, :LANES]
                yf[i : i + 1, :] = plane[y1 : y1 + 1, :LANES]
                columns[0] = jnp.where(lane == i, moved, columns[0])
            else:
                xf[0:y1, :] = plane[:y1, :LANES]
                xy[0:1, :] = plane[y1 : y1 + 1, :LANES]
                corners = [jnp.where(lane == 0, moved, 0.0)]
            if i % 2 or i == x1:
                stages[0][i // 2, PAD : PAD + rows, :] = fold_x(comps, i // 2, p.xs[1])

    grids = [None]
    for l in range(1, LEVELS):
        n, e = p.xs[l], p.ext[l]
        planes = [fold_y(stages[l - 1], k, e) for k in range(n + 1)]
        lane = lanes_of(e)
        for k in range(n + 1):
            to = p.zoff[l] + k % n
            moved = roll(planes[k], to - p.tail[l])
            if k < n:
                columns[l] = jnp.where(lane == to, moved, columns[l])
            else:
                corners.append(jnp.where(lane == to, moved, 0.0))
        grids.append(planes)
        if l + 1 < LEVELS:
            for k in range(p.xs[l + 1] + 1):
                stages[l][k, PAD : PAD + e, :] = fold_x(planes, k, p.xs[l + 1])

    def pick(pieces):
        n = pieces[0][1].shape[0]
        lane = lanes_of(n)
        out = pieces[0][1]
        for l, x in pieces[1:]:
            out = jnp.where(lane >= p.coff[l], x, out)
        return out

    def face(cols, dst, edge):
        for g in range(y1 // 8):
            dst[8 * g : 8 * g + 8, :] = functools.reduce(
                jnp.add, [t[8 * g : 8 * g + 8] for t in cols if 8 * g + 8 <= t.shape[0]]
            )
        line = functools.reduce(
            jnp.add, [t[y : y + 1] for t, y in zip(cols, p.ys)]
        )
        top = lax.broadcasted_iota(jnp.int32, (8, LANES), 0) == 0
        edge[...] = jnp.where(top, line, 0.0)

    face(corners, zx, xyz)
    face(columns, zf, yz)
    levels = range(1, LEVELS)
    for g in range(p.pys[1] // 8):
        at = y1 + 8 * g
        xf[at : at + 8, :] = pick(
            [
                (l, grids[l][p.xs[l]][8 * g : 8 * g + 8])
                for l in levels
                if 8 * g + 8 <= p.pys[l]
            ]
        )
    xy[1:2, :] = pick([(l, grids[l][p.xs[l]][p.ys[l] : p.ys[l] + 1]) for l in levels])
    for k in range(p.xs[1]):
        yf[x1 + k : x1 + k + 1, :] = pick(
            [(l, grids[l][k][p.ys[l] : p.ys[l] + 1]) for l in levels if k < p.xs[l]]
        )
    for l in levels:
        q = p.pys[l]
        for k in range(p.xs[l]):
            outc[p.base[l] + k * q : p.base[l] + (k + 1) * q, :] = grids[l][k][:q]

    pl.semaphore_wait(barrier, len(others))

    has_next, has_prev, copies = [], [], []
    for n, hop in enumerate(HOPS):
        ok_n, target = along(hop, 1)
        has_next.append(ok_n)
        has_prev.append(along(hop, -1)[0])
        copies.append(
            pltpu.make_async_remote_copy(
                src_ref=sends[n],
                dst_ref=recvs[n],
                send_sem=ssem.at[n],
                recv_sem=rsem.at[n],
                device_id=target,
                device_id_type=MESH,
            )
        )
    for n in range(len(HOPS)):

        @pl.when(has_next[n])
        def _():
            copies[n].start()

    for n in range(len(HOPS)):

        @pl.when(jnp.logical_not(has_prev[n]))
        def _():
            recvs[n][...] = jnp.zeros(recvs[n].shape, f32)

    for n in range(len(HOPS)):

        @pl.when(has_prev[n])
        def _():
            copies[n].wait_recv()

    rxyz, rzx, ryz, rzf, rxf, rxy, ryf = recvs
    col = [rzf[8 * g : 8 * g + 8, :] + rzx[8 * g : 8 * g + 8, :] for g in range(y1 // 8)]
    col[0] = col[0] + ryz[...] + rxyz[...]
    top = lax.broadcasted_iota(jnp.int32, (8, LANES), 0) == 0
    row = lax.broadcasted_iota(jnp.int32, (8, LANES), 0)
    lane = lanes_of(8)
    acc = jnp.zeros((8, LANES), f32)
    for i in range(x1):
        edge = ryf[i : i + 1, :]
        if i == 0:
            edge = edge + rxy[0:1, :]
        for g in range(y1 // 8):
            part = out1[i, 8 * g : 8 * g + 8, :]
            if i == 0:
                part = part + rxf[8 * g : 8 * g + 8, :]
            if g == 0:
                part = part + jnp.where(top, edge, 0.0)
            part = part + jnp.where(lane == 0, roll(col[g], -i), 0.0)
            out1[i, 8 * g : 8 * g + 8, :] = part
            acc = acc + part * part
    results = [
        pltpu.make_async_copy(out1, out1_hbm, osem.at[0]),
        pltpu.make_async_copy(outc, outc_hbm, osem.at[1]),
    ]
    results[0].start()
    mine[0:1, :] = jnp.sum(acc, axis=0, keepdims=True)
    acc = jnp.zeros((8, LANES), f32)
    for l in levels:
        q = p.pys[l]
        keep = (lane >= p.coff[l]) & (lane < p.coff[l + 1] if l + 1 < LEVELS else lane < p.end)
        if p.ys[l] < 8:
            keep = keep & (row < p.ys[l])
        total = jnp.zeros((8, LANES), f32)
        for k in range(p.xs[l]):
            edge = ryf[x1 + k : x1 + k + 1, :]
            if k == 0:
                edge = edge + rxy[1:2, :]
            for g in range(q // 8):
                at = p.base[l] + k * q + 8 * g
                part = outc[at : at + 8, :]
                if k == 0:
                    part = part + rxf[y1 + 8 * g : y1 + 8 * g + 8, :]
                if g == 0:
                    part = part + jnp.where(top, edge, 0.0)
                shifted = roll(col[g], p.coff[l] - p.zoff[l] - k)
                part = part + jnp.where(lane == p.coff[l], shifted, 0.0)
                outc[at : at + 8, :] = part
                total = total + part * part
        acc = jnp.where(keep, total, acc)
    mine[1:2, :] = jnp.sum(acc, axis=0, keepdims=True)
    results[1].start()

    pending = [
        pltpu.make_async_remote_copy(
            src_ref=mine,
            dst_ref=parts.at[k + 1],
            send_sem=asend.at[k],
            recv_sem=arecv.at[k],
            device_id=target,
            device_id_type=MESH,
        )
        for k, target in enumerate(others)
    ]
    for c in reversed(pending):
        c.start()
    parts[0] = mine[...]
    for c in pending:
        c.wait_recv()
    stats[...] = jnp.sum(parts[...], axis=0)
    for c in results:
        c.wait()
    for c in pending:
        c.wait_send()
    for n in range(len(HOPS)):

        @pl.when(has_next[n])
        def _():
            copies[n].wait_send()


def scale_kernel(plan, devices, grid, packed, stats, o1, o2, o3, o4, o5, scales):
    p = plan
    lane1 = lax.broadcasted_iota(jnp.int32, (1, LANES), 1)
    outs = (o1, o2, o3, o4, o5)
    product = jnp.ones((1, 1), jnp.float32)
    for l in range(LEVELS):
        row = stats[0:1, :] if l == 0 else stats[1:2, :]
        if l:
            end = p.coff[l] + p.zs[l]
            row = jnp.where((lane1 >= p.coff[l]) & (lane1 < end), row, 0.0)
        total = jnp.sum(row, axis=1, keepdims=True)
        cells = devices * p.xs[l] * p.ys[l] * p.zs[l]
        scale = jnp.sqrt(total / (product * product) / cells + EPSILON)
        product = product * scale
        scales[l] = scale[0, 0]
        inverse = 1.0 / product
        if l == 0:
            o1[...] = grid[...] * inverse.reshape(1, 1, 1)
            continue
        block = packed[p.base[l] : p.base[l + 1], :] * inverse
        block = roll(block, -p.coff[l])
        block = block.reshape(p.xs[l], p.pys[l], LANES)
        outs[l][...] = block[:, : p.ys[l], : p.zs[l]]


def per_device(sizes, residual_in):
    plan = Plan(residual_in.shape)
    p = plan
    count = sizes[0] * sizes[1] * sizes[2]
    f32, bf16 = jnp.float32, jnp.bfloat16
    long = p.ys[0] + p.pys[1]
    messages = [(8, LANES), (p.ys[0], LANES), (8, LANES), (p.ys[0], LANES)]
    messages += [(long, LANES), (8, LANES), (p.xs[0] + p.xs[1], LANES)]
    anywhere = pl.BlockSpec(memory_space=pl.ANY)
    vmem = pl.BlockSpec(memory_space=pltpu.VMEM)
    dma = pltpu.SemaphoreType.DMA
    grid, packed, stats = pl.pallas_call(
        functools.partial(gather_kernel, p, sizes),
        out_shape=(
            jax.ShapeDtypeStruct((p.xs[0], p.ys[0], p.zs[0]), f32),
            jax.ShapeDtypeStruct((p.own, LANES), f32),
            jax.ShapeDtypeStruct((2, LANES), f32),
        ),
        in_specs=[anywhere] * 2,
        out_specs=(anywhere, anywhere, vmem),
        scratch_shapes=[
            pltpu.VMEM((p.nx, 2, p.ny + 3 * PAD, LANES), f32),
            pltpu.VMEM((p.nz, 2 * LANES), bf16),
        ]
        + [pltpu.VMEM((p.xs[l] + 1, p.stage[l - 1], LANES), f32) for l in range(1, LEVELS)]
        + [pltpu.VMEM(s, f32) for s in messages]
        + [pltpu.VMEM(s, f32) for s in messages]
        + [
            pltpu.VMEM((2, LANES), f32),
            pltpu.VMEM((count, 2, LANES), f32),
            dma((2 * CHUNKS,)),
            dma((1,)),
            dma((len(HOPS),)),
            dma((len(HOPS),)),
            dma((count - 1,)),
            dma((count - 1,)),
            pltpu.VMEM((p.xs[0], p.ys[0], p.zs[0]), f32),
            pltpu.VMEM((p.own, LANES), f32),
            dma((2,)),
        ],
        compiler_params=pltpu.CompilerParams(collective_id=0, has_side_effects=True),
        name="restrict_exchange",
    )(residual_in, jnp.asarray(p.table()))
    shapes = list(zip(p.xs, p.ys, p.zs))
    return pl.pallas_call(
        functools.partial(scale_kernel, p, count),
        out_shape=tuple(jax.ShapeDtypeStruct(s, f32) for s in shapes)
        + (jax.ShapeDtypeStruct((LEVELS,), f32),),
        in_specs=[vmem] * 3,
        out_specs=(vmem,) * 5 + (pl.BlockSpec(memory_space=pltpu.SMEM),),
        name="scale_levels",
    )(grid, packed, stats)


def solution(mesh):
    sizes = tuple(mesh.shape[a] for a in AXES)
    spec = P(*AXES)
    return jax.shard_map(
        functools.partial(per_device, sizes),
        mesh=mesh,
        in_specs=(spec,),
        out_specs=(spec,) * 5 + (P(),),
        check_vma=False,
    )
```

time: 23 us -> 18.8 us (0.82)
  Pallas kernels: 22.2 us -> 18 us
    pallas_call x1, Pallas kernels: 20.1 us -> 15.9 us  [per_device(): pl.pallas_call(functools.partial(gather_kernel, p, sizes), out_shape=(jax...]
where the time goes in v1:
time: 18.8 us; the launch traced here: 18.7 us
  Pallas kernels  18 us (96%)
  between operations  0.64 us (3%)
    pallas_call x1, Pallas kernels, per_device(): pl.pallas_call(functools.partial(gather_kernel, p, sizes), out_shape=(jax...  15.9 us
    pallas_call x1, Pallas kernels, per_device(): pl.pallas_call(functools.partial(scale_kernel, p, count), out_shape=tuple...  2.13 us

profile of v1, /device:TPU:0, one launch (start us, length us, event | category | flops | bytes accessed | tf_op | source)
XLA Modules:
  0.0 18.7 jit_solution(17566368048707036740)
XLA Ops:
  0.6 15.9 %restrict_exchange.1 = (f32[32,32,128]{2,1,0:T(8,128)}, f32[368,128]{1,0:T(8,128)}, f32[2,128]{1,0:T(2,128)}) custom-call(f32[64,64,256]{2,1,0:T(8,128)} %refs_0_.1, bf16[256,256]{1,0:T(8,128)(2,1)} %constant.2.clone.refs_1_), custom_call_target="tpu_custom_call" | custom-call | tf_op jit(solution)/shard_map/restrict_exchange/pallas_call | solution.py:438
  16.5 2.1 %scale_levels.1 = (f32[32,32,128]{2,1,0:T(8,128)}, f32[16,16,64]{2,1,0:T(8,128)}, f32[8,8,32]{2,1,0:T(8,128)}, f32[4,4,16]{2,1,0:T(4,128)}, f32[2,2,8]{2,1,0:T(2,128)}, /*index=5*/f32[5]{0:T(128)}) custom-call(f32[32,32,128]{2,1,0:T(8,128)} %get-tuple-element.9.grid, f32[368,128]{1,0:T(8,128)} %get-tuple-element.10.packed, f32[2,128]{1,0:T(2,128)} %get-tuple-element.11.stats), custom_call_target="tpu_custom_call" | custom-call | tf_op jit(solution)/shard_map/scale_levels/pallas_call | solution.py:471

commit v2 on v1

--- a/solution.py
+++ b/solution.py
@@ -2,7 +2,6 @@
 
 import jax
 import jax.numpy as jnp
-import ml_dtypes
 import numpy as np
 from jax import lax
 from jax.experimental import pallas as pl
@@ -21,21 +20,6 @@
 
 def round_up(n, m):
     return -(-n // m) * m
-
-
-def step_matrix(n_in, n_cells):
-    out = np.zeros((n_cells // 2 + 1, n_in))
-    for i in range(n_cells // 2 + 1):
-        for off, w in ((-1, 0.25), (0, 0.5), (1, 0.25)):
-            if 0 <= 2 * i + off < n_in:
-                out[i, 2 * i + off] = w
-    return out
-
-
-def exact(table):
-    out = table.astype(np.float32).astype(ml_dtypes.bfloat16)
-    assert (out.astype(np.float64) == table).all()
-    return out
 
 
 class Plan:
@@ -58,17 +42,26 @@
         self.own = self.base[-1]
         self.stage = [PAD + max(self.ext[l - 1], 2 * self.ext[l]) for l in range(1, LEVELS)]
 
-    def table(self):
-        m = step_matrix(self.nz, self.nz)
-        out = np.zeros((self.nz, 2 * LANES))
-        out[:, :LANES] = m[:-1].T
-        out[:, LANES + self.tail[0]] = m[-1]
+    def fill(self, table):
+        col = lax.broadcasted_iota(jnp.int32, (1, 2 * LANES), 1)
+        width = jnp.full((1, 2 * LANES), 2, jnp.int32)
+        cell = col
         for l in range(1, LEVELS):
-            m = step_matrix(self.zs[l - 1] + 1, self.zs[l - 1]) @ m
-            at = LANES + self.coff[l]
-            out[:, at : at + self.zs[l]] = m[:-1].T
-            out[:, LANES + self.tail[l]] = m[-1]
-        return exact(out / 16)
+            inside = col >= LANES + self.coff[l]
+            width = jnp.where(inside, 2 << l, width)
+            cell = jnp.where(inside, col - (LANES + self.coff[l]), cell)
+        for l in range(LEVELS):
+            inside = col == LANES + self.tail[l]
+            width = jnp.where(inside, 2 << l, width)
+            cell = jnp.where(inside, self.zs[l], cell)
+        inside = (col < LANES + self.end + LEVELS).astype(jnp.float32)
+        at, width = (width * cell).astype(jnp.float32), width.astype(jnp.float32)
+        factor = inside / (16.0 * width * width)
+        step = 64
+        for r in range(0, self.nz, step):
+            z = lax.broadcasted_iota(jnp.int32, (step, 2 * LANES), 0) + r
+            hat = jnp.maximum(width - jnp.abs(z.astype(jnp.float32) - at), 0.0)
+            table[r : r + step, :] = (hat * factor).astype(jnp.bfloat16)
 
 
 def halves(x):
@@ -87,15 +80,14 @@
 
 def gather_kernel(plan, sizes, *refs):
     p = plan
-    v_hbm, table_hbm = refs[:2]
-    out1_hbm, outc_hbm, stats = refs[2:5]
-    vin, table = refs[5:7]
-    stages = refs[7:11]
-    sends = refs[11:18]
-    recvs = refs[18:25]
-    mine, parts = refs[25:27]
-    vsem, tsem, ssem, rsem, asend, arecv = refs[27:33]
-    out1, outc, osem = refs[33:36]
+    v_hbm = refs[0]
+    out1, outc, stats = refs[1:4]
+    vin, table = refs[4:6]
+    stages = refs[6:10]
+    sends = refs[10:17]
+    recvs = refs[17:24]
+    mine, parts = refs[24:26]
+    vsem, ssem, rsem, asend, arecv = refs[26:31]
     f32 = jnp.float32
     pos = [lax.axis_index(a) for a in AXES]
     group = sizes[0] * sizes[1]
@@ -122,7 +114,6 @@
         return ok, target
 
     per = p.nx // CHUNKS
-    tcopy = pltpu.make_async_copy(table_hbm, table, tsem.at[0])
     vcopies = [
         [
             pltpu.make_async_copy(
@@ -134,11 +125,7 @@
         ]
         for c in range(CHUNKS)
     ]
-    for pair in vcopies[:1]:
-        for c in pair:
-            c.start()
-    tcopy.start()
-    for pair in vcopies[1:]:
+    for pair in vcopies:
         for c in pair:
             c.start()
 
@@ -146,6 +133,7 @@
     for target in others:
         pl.semaphore_signal(barrier, inc=1, device_id=target, device_id_type=MESH)
 
+    p.fill(table)
     after = PAD + p.ny
     for x in range(p.nx):
         for h in range(2):
@@ -191,7 +179,6 @@
     comps = []
     columns = [jnp.zeros((e, LANES), f32) for e in p.ext]
     before = None
-    tcopy.wait()
     for c in range(CHUNKS):
         for copy in vcopies[c]:
             copy.wait()
@@ -339,11 +326,6 @@
             part = part + jnp.where(lane == 0, roll(col[g], -i), 0.0)
             out1[i, 8 * g : 8 * g + 8, :] = part
             acc = acc + part * part
-    results = [
-        pltpu.make_async_copy(out1, out1_hbm, osem.at[0]),
-        pltpu.make_async_copy(outc, outc_hbm, osem.at[1]),
-    ]
-    results[0].start()
     mine[0:1, :] = jnp.sum(acc, axis=0, keepdims=True)
     acc = jnp.zeros((8, LANES), f32)
     for l in levels:
@@ -369,7 +351,6 @@
                 total = total + part * part
         acc = jnp.where(keep, total, acc)
     mine[1:2, :] = jnp.sum(acc, axis=0, keepdims=True)
-    results[1].start()
 
     pending = [
         pltpu.make_async_remote_copy(
@@ -388,8 +369,6 @@
     for c in pending:
         c.wait_recv()
     stats[...] = jnp.sum(parts[...], axis=0)
-    for c in results:
-        c.wait()
     for c in pending:
         c.wait_send()
     for n in range(len(HOPS)):
@@ -442,8 +421,8 @@
             jax.ShapeDtypeStruct((p.own, LANES), f32),
             jax.ShapeDtypeStruct((2, LANES), f32),
         ),
-        in_specs=[anywhere] * 2,
-        out_specs=(anywhere, anywhere, vmem),
+        in_specs=[anywhere],
+        out_specs=(vmem, vmem, vmem),
         scratch_shapes=[
             pltpu.VMEM((p.nx, 2, p.ny + 3 * PAD, LANES), f32),
             pltpu.VMEM((p.nz, 2 * LANES), bf16),
@@ -455,18 +434,16 @@
             pltpu.VMEM((2, LANES), f32),
             pltpu.VMEM((count, 2, LANES), f32),
             dma((2 * CHUNKS,)),
-            dma((1,)),
             dma((len(HOPS),)),
             dma((len(HOPS),)),
             dma((count - 1,)),
             dma((count - 1,)),
-            pltpu.VMEM((p.xs[0], p.ys[0], p.zs[0]), f32),
-            pltpu.VMEM((p.own, LANES), f32),
-            dma((2,)),
         ],
-        compiler_params=pltpu.CompilerParams(collective_id=0, has_side_effects=True),
+        compiler_params=pltpu.CompilerParams(
+            collective_id=0, has_side_effects=True, vmem_limit_bytes=51 << 20
+        ),
         name="restrict_exchange",
-    )(residual_in, jnp.asarray(p.table()))
+    )(residual_in)
     shapes = list(zip(p.xs, p.ys, p.zs))
     return pl.pallas_call(
         functools.partial(scale_kernel, p, count),
@@ -474,6 +451,7 @@
         + (jax.ShapeDtypeStruct((LEVELS,), f32),),
         in_specs=[vmem] * 3,
         out_specs=(vmem,) * 5 + (pl.BlockSpec(memory_space=pltpu.SMEM),),
+        compiler_params=pltpu.CompilerParams(vmem_limit_bytes=8 << 20),
         name="scale_levels",
     )(grid, packed, stats)
 

time: 18.8 us -> 17.1 us (0.910)
  Pallas kernels: 18 us -> 16.3 us
    pallas_call x1, Pallas kernels: 2.13 us -> 0.99 us  [per_device(): pl.pallas_call(functools.partial(scale_kernel, p, count), out_shape=tuple...]
    pallas_call x1, Pallas kernels: 15.9 us -> 15.3 us  [per_device(): pl.pallas_call(functools.partial(gather_kernel, p, sizes), out_shape=(jax...]
where the time goes in v2:
time: 17.1 us; the launch traced here: 16.9 us
  Pallas kernels  16.3 us (95%)
  between operations  0.64 us (4%)
    pallas_call x1, Pallas kernels, per_device(): pl.pallas_call(functools.partial(gather_kernel, p, sizes), out_shape=(jax...  15.3 us
    pallas_call x1, Pallas kernels, per_device(): pl.pallas_call(functools.partial(scale_kernel, p, count), out_shape=tuple...  0.99 us

profile of v2, /device:TPU:0, one launch (start us, length us, event | category | flops | bytes accessed | tf_op | source)
XLA Modules:
  0.0 16.9 jit_solution(1891524229825314556)
XLA Ops:
  0.6 15.3 %restrict_exchange.1 = (f32[32,32,128]{2,1,0:T(8,128)S(1)}, f32[368,128]{1,0:T(8,128)S(1)}, f32[2,128]{1,0:T(2,128)S(1)}) custom-call(f32[64,64,256]{2,1,0:T(8,128)} %refs_0_.1), custom_call_target="tpu_custom_call" | custom-call | tf_op jit(solution)/shard_map/restrict_exchange/pallas_call | solution.py:417
  15.9 1.0 %scale_levels.1 = (f32[32,32,128]{2,1,0:T(8,128)}, f32[16,16,64]{2,1,0:T(8,128)}, f32[8,8,32]{2,1,0:T(8,128)}, f32[4,4,16]{2,1,0:T(4,128)}, f32[2,2,8]{2,1,0:T(2,128)}, /*index=5*/f32[5]{0:T(128)}) custom-call(f32[32,32,128]{2,1,0:T(8,128)S(1)} %get-tuple-element.9.grid, f32[368,128]{1,0:T(8,128)S(1)} %get-tuple-element.10.packed, ...), custom_call_target="tpu_custom_call" | custom-call | tf_op jit(solution)/shard_map/scale_levels/pallas_call | solution.py:448

commit v3 on v2

--- a/solution.py
+++ b/solution.py
@@ -35,8 +35,12 @@
         self.end = self.coff[-1]
         self.tail = [self.end + LEVELS - 1] + [self.end + l for l in range(LEVELS - 1)]
         assert self.end + LEVELS <= LANES
-        self.zoff = np.concatenate([[0], np.cumsum(self.xs)]).tolist()
-        assert self.zoff[-1] <= LANES
+        self.zoff = [0, 1]
+        for l in range(1, LEVELS):
+            self.zoff.append(self.zoff[l] + self.xs[l] * self.pys[l] // 8)
+        assert self.xs[0] * self.ys[0] // 8 <= LANES and self.zoff[-1] <= self.xs[0] * 2
+        firsts = [self.zoff[l] + g * self.xs[l] for l in range(1, LEVELS) for g in range(self.pys[l] // 8)]
+        assert all(f % self.xs[0] for f in firsts)
         rows = [x * p for x, p in zip(self.xs[1:], self.pys[1:])]
         self.base = [0] + np.concatenate([[0], np.cumsum(rows)]).tolist()
         self.own = self.base[-1]
@@ -175,10 +179,32 @@
     xyz, zx, yz, zf, xf, xy, yf = sends
     half = per // 2
     rows = p.ext[0]
-    lane = lanes_of(rows)
     comps = []
-    columns = [jnp.zeros((e, LANES), f32) for e in p.ext]
+    lane = lanes_of(8)
+    row = lax.broadcasted_iota(jnp.int32, (8, LANES), 0)
+    blank = jnp.zeros((8, LANES), f32)
+    faces = {"zf": [blank, blank], "zx": [blank, blank], "yz": [], "xyz": []}
+
+    def collect(l, planes, first, line):
+        n, block = p.xs[l], min(l, 1)
+        for i, plane in enumerate(planes, first):
+            z, y = ("zf", "yz") if i < n else ("zx", "xyz")
+            for g in range(p.pys[l] // 8):
+                to = p.zoff[l] + g * n + i % n
+                moved = roll(plane[8 * g : 8 * g + 8], to - p.tail[l])
+                faces[z][block] = jnp.where(lane == to, moved, faces[z][block])
+            to = p.zoff[l] + i % n
+            g = p.ys[l] // 8
+            moved = roll(plane[8 * g : 8 * g + 8], to - p.tail[l])
+            line[y] = jnp.where(lane == to, moved, line[y])
+
+    def close(l, line):
+        s = p.ys[l] % 8
+        for y in ("yz", "xyz"):
+            faces[y].append(line[y][s : s + 1])
+
     before = None
+    line = {"yz": blank, "xyz": blank}
     for c in range(CHUNKS):
         for copy in vcopies[c]:
             copy.wait()
@@ -201,30 +227,24 @@
             plane = z[j * rows : (j + 1) * rows]
             comp = plane[:, LANES:]
             comps.append(comp)
-            moved = roll(comp, (i % x1) - p.tail[0])
+            collect(0, [comp], i, line)
             if i < x1:
                 out1[i] = plane[:y1, :LANES]
                 yf[i : i + 1, :] = plane[y1 : y1 + 1, :LANES]
-                columns[0] = jnp.where(lane == i, moved, columns[0])
             else:
                 xf[0:y1, :] = plane[:y1, :LANES]
                 xy[0:1, :] = plane[y1 : y1 + 1, :LANES]
-                corners = [jnp.where(lane == 0, moved, 0.0)]
             if i % 2 or i == x1:
                 stages[0][i // 2, PAD : PAD + rows, :] = fold_x(comps, i // 2, p.xs[1])
 
+    close(0, line)
     grids = [None]
     for l in range(1, LEVELS):
         n, e = p.xs[l], p.ext[l]
         planes = [fold_y(stages[l - 1], k, e) for k in range(n + 1)]
-        lane = lanes_of(e)
-        for k in range(n + 1):
-            to = p.zoff[l] + k % n
-            moved = roll(planes[k], to - p.tail[l])
-            if k < n:
-                columns[l] = jnp.where(lane == to, moved, columns[l])
-            else:
-                corners.append(jnp.where(lane == to, moved, 0.0))
+        line = {"yz": blank, "xyz": blank}
+        collect(l, planes, 0, line)
+        close(l, line)
         grids.append(planes)
         if l + 1 < LEVELS:
             for k in range(p.xs[l + 1] + 1):
@@ -238,19 +258,12 @@
             out = jnp.where(lane >= p.coff[l], x, out)
         return out
 
-    def face(cols, dst, edge):
-        for g in range(y1 // 8):
-            dst[8 * g : 8 * g + 8, :] = functools.reduce(
-                jnp.add, [t[8 * g : 8 * g + 8] for t in cols if 8 * g + 8 <= t.shape[0]]
-            )
-        line = functools.reduce(
-            jnp.add, [t[y : y + 1] for t, y in zip(cols, p.ys)]
-        )
-        top = lax.broadcasted_iota(jnp.int32, (8, LANES), 0) == 0
-        edge[...] = jnp.where(top, line, 0.0)
-
-    face(corners, zx, xyz)
-    face(columns, zf, yz)
+    zf[0:8, :] = faces["zf"][0]
+    zf[8:16, :] = faces["zf"][1]
+    zx[...] = faces["zx"][0] + faces["zx"][1]
+    for name, ref in (("yz", yz), ("xyz", xyz)):
+        ref[0:1, :] = faces[name][0]
+        ref[1:2, :] = functools.reduce(jnp.add, faces[name][1:])
     levels = range(1, LEVELS)
     for g in range(p.pys[1] // 8):
         at = y1 + 8 * g
@@ -307,11 +320,11 @@
             copies[n].wait_recv()
 
     rxyz, rzx, ryz, rzf, rxf, rxy, ryf = recvs
-    col = [rzf[8 * g : 8 * g + 8, :] + rzx[8 * g : 8 * g + 8, :] for g in range(y1 // 8)]
-    col[0] = col[0] + ryz[...] + rxyz[...]
-    top = lax.broadcasted_iota(jnp.int32, (8, LANES), 0) == 0
-    row = lax.broadcasted_iota(jnp.int32, (8, LANES), 0)
-    lane = lanes_of(8)
+    top = row == 0
+    mine_first = lane % x1 == 0
+    lines = ryz[...] + rxyz[...]
+    col1 = rzf[0:8, :] + jnp.where(mine_first, rzx[...], 0.0) + jnp.where(top, lines[0:1], 0.0)
+    col2 = rzf[8:16, :] + jnp.where(mine_first, 0.0, rzx[...]) + jnp.where(top, lines[1:2], 0.0)
     acc = jnp.zeros((8, LANES), f32)
     for i in range(x1):
         edge = ryf[i : i + 1, :]
@@ -323,7 +336,7 @@
                 part = part + rxf[8 * g : 8 * g + 8, :]
             if g == 0:
                 part = part + jnp.where(top, edge, 0.0)
-            part = part + jnp.where(lane == 0, roll(col[g], -i), 0.0)
+            part = part + jnp.where(lane == 0, roll(col1, -(g * x1 + i)), 0.0)
             out1[i, 8 * g : 8 * g + 8, :] = part
             acc = acc + part * part
     mine[0:1, :] = jnp.sum(acc, axis=0, keepdims=True)
@@ -345,7 +358,7 @@
                     part = part + rxf[y1 + 8 * g : y1 + 8 * g + 8, :]
                 if g == 0:
                     part = part + jnp.where(top, edge, 0.0)
-                shifted = roll(col[g], p.coff[l] - p.zoff[l] - k)
+                shifted = roll(col2, p.coff[l] - p.zoff[l] - g * p.xs[l] - k)
                 part = part + jnp.where(lane == p.coff[l], shifted, 0.0)
                 outc[at : at + 8, :] = part
                 total = total + part * part
@@ -356,8 +369,8 @@
         pltpu.make_async_remote_copy(
             src_ref=mine,
             dst_ref=parts.at[k + 1],
-            send_sem=asend.at[k],
-            recv_sem=arecv.at[k],
+            send_sem=asend.at[0],
+            recv_sem=arecv.at[0],
             device_id=target,
             device_id_type=MESH,
         )
@@ -366,11 +379,17 @@
     for c in reversed(pending):
         c.start()
     parts[0] = mine[...]
-    for c in pending:
-        c.wait_recv()
+    every = pltpu.make_async_remote_copy(
+        src_ref=parts.at[pl.ds(1, len(others))],
+        dst_ref=parts.at[pl.ds(1, len(others))],
+        send_sem=asend.at[0],
+        recv_sem=arecv.at[0],
+        device_id=others[0],
+        device_id_type=MESH,
+    )
+    every.wait_recv()
     stats[...] = jnp.sum(parts[...], axis=0)
-    for c in pending:
-        c.wait_send()
+    every.wait_send()
     for n in range(len(HOPS)):
 
         @pl.when(has_next[n])
@@ -382,18 +401,17 @@
     p = plan
     lane1 = lax.broadcasted_iota(jnp.int32, (1, LANES), 1)
     outs = (o1, o2, o3, o4, o5)
-    product = jnp.ones((1, 1), jnp.float32)
+    square = jnp.ones((1, 1), jnp.float32)
     for l in range(LEVELS):
         row = stats[0:1, :] if l == 0 else stats[1:2, :]
         if l:
             end = p.coff[l] + p.zs[l]
             row = jnp.where((lane1 >= p.coff[l]) & (lane1 < end), row, 0.0)
-        total = jnp.sum(row, axis=1, keepdims=True)
         cells = devices * p.xs[l] * p.ys[l] * p.zs[l]
-        scale = jnp.sqrt(total / (product * product) / cells + EPSILON)
-        product = product * scale
-        scales[l] = scale[0, 0]
-        inverse = 1.0 / product
+        mean = jnp.sum(row, axis=1, keepdims=True) * (1.0 / cells)
+        before, square = square, mean + EPSILON * square
+        scales[l] = jnp.sqrt(square / before)[0, 0]
+        inverse = 1.0 / jnp.sqrt(square)
         if l == 0:
             o1[...] = grid[...] * inverse.reshape(1, 1, 1)
             continue
@@ -409,8 +427,8 @@
     count = sizes[0] * sizes[1] * sizes[2]
     f32, bf16 = jnp.float32, jnp.bfloat16
     long = p.ys[0] + p.pys[1]
-    messages = [(8, LANES), (p.ys[0], LANES), (8, LANES), (p.ys[0], LANES)]
-    messages += [(long, LANES), (8, LANES), (p.xs[0] + p.xs[1], LANES)]
+    messages = [(2, LANES), (8, LANES), (2, LANES), (16, LANES)]
+    messages += [(long, LANES), (2, LANES), (p.xs[0] + p.xs[1], LANES)]
     anywhere = pl.BlockSpec(memory_space=pl.ANY)
     vmem = pl.BlockSpec(memory_space=pltpu.VMEM)
     dma = pltpu.SemaphoreType.DMA
@@ -436,8 +454,8 @@
             dma((2 * CHUNKS,)),
             dma((len(HOPS),)),
             dma((len(HOPS),)),
-            dma((count - 1,)),
-            dma((count - 1,)),
+            dma((1,)),
+            dma((1,)),
         ],
         compiler_params=pltpu.CompilerParams(
             collective_id=0, has_side_effects=True, vmem_limit_bytes=51 << 20

time: 17.1 us -> 16.3 us (0.953)
  Pallas kernels: 16.3 us -> 15.5 us
    pallas_call x1, Pallas kernels: 15.3 us -> 14.6 us  [per_device(): pl.pallas_call(functools.partial(gather_kernel, p, sizes), out_shape=(jax...]
where the time goes in v3:
time: 16.3 us; the launch traced here: 16.2 us
  Pallas kernels  15.5 us (95%)
  between operations  0.64 us (4%)
    pallas_call x1, Pallas kernels, per_device(): pl.pallas_call(functools.partial(gather_kernel, p, sizes), out_shape=(jax...  14.6 us
    pallas_call x1, Pallas kernels, per_device(): pl.pallas_call(functools.partial(scale_kernel, p, count), out_shape=tuple...  0.99 us

profile of v3, /device:TPU:0, one launch (start us, length us, event | category | flops | bytes accessed | tf_op | source)
XLA Modules:
  0.0 16.2 jit_solution(12878932380301047326)
XLA Ops:
  0.6 14.6 %restrict_exchange.1 = (f32[32,32,128]{2,1,0:T(8,128)S(1)}, f32[368,128]{1,0:T(8,128)S(1)}, f32[2,128]{1,0:T(2,128)S(1)}) custom-call(f32[64,64,256]{2,1,0:T(8,128)} %refs_0_.1), custom_call_target="tpu_custom_call" | custom-call | tf_op jit(solution)/shard_map/restrict_exchange/pallas_call | solution.py:435
  15.2 1.0 %scale_levels.1 = (f32[32,32,128]{2,1,0:T(8,128)}, f32[16,16,64]{2,1,0:T(8,128)}, f32[8,8,32]{2,1,0:T(8,128)}, f32[4,4,16]{2,1,0:T(4,128)}, f32[2,2,8]{2,1,0:T(2,128)}, /*index=5*/f32[5]{0:T(128)}) custom-call(f32[32,32,128]{2,1,0:T(8,128)S(1)} %get-tuple-element.9.grid, f32[368,128]{1,0:T(8,128)S(1)} %get-tuple-element.10.packed, ...), custom_call_target="tpu_custom_call" | custom-call | tf_op jit(solution)/shard_map/scale_levels/pallas_call | solution.py:466

commit v4 on v3

--- a/solution.py
+++ b/solution.py
@@ -12,7 +12,7 @@
 EPSILON = 1e-06
 LANES = 128
 PAD = 8
-CHUNKS = 4
+CHUNKS = (1, 1)
 AXES = ("gx", "gy", "gz")
 MESH = pl.DeviceIdType.MESH
 HOPS = ((1, 1, 1), (1, 0, 1), (0, 1, 1), (0, 0, 1), (1, 0, 0), (1, 1, 0), (0, 1, 0))
@@ -102,10 +102,19 @@
     for k in range(group):
         r = lax.rem(me + k, group)
         in_plane.append((r // sizes[1], lax.rem(r, sizes[1])))
-    in_line = [lax.rem(pos[2] + k, sizes[2]) for k in range(sizes[2])]
-    others = [
-        {"gx": gx, "gy": gy, "gz": gz} for gz in in_line for gx, gy in in_plane
-    ][1:]
+    others, slots = [], []
+    for k in range(sizes[2]):
+        rest = sizes[2] - 1 - k
+        gz = pos[2]
+        if rest:
+            low = k + (k >= pos[2]).astype(jnp.int32)
+            high = rest - (rest <= pos[2]).astype(jnp.int32)
+            gz = jnp.where(2 * pos[2] >= sizes[2], low, high)
+        slot = lax.rem(gz - pos[2] + sizes[2], sizes[2]) * group
+        for n in reversed(range(0 if rest else 1, group)):
+            gx, gy = in_plane[n]
+            others.append({"gx": gx, "gy": gy, "gz": gz})
+            slots.append(slot + n)
 
     def along(hop, way):
         ok, target = None, {}
@@ -117,17 +126,19 @@
                 target[AXES[a]] = lax.rem(pos[a] + way + sizes[a], sizes[a])
         return ok, target
 
-    per = p.nx // CHUNKS
+    unit = p.nx // sum(CHUNKS)
+    starts = [unit * sum(CHUNKS[:c]) for c in range(len(CHUNKS) + 1)]
+    spans = [pl.ds(a, b - a) for a, b in zip(starts, starts[1:])]
     vcopies = [
         [
             pltpu.make_async_copy(
-                v_hbm.at[pl.ds(c * per, per), :, pl.ds(h * LANES, LANES)],
-                vin.at[pl.ds(c * per, per), h, pl.ds(PAD, p.ny)],
+                v_hbm.at[span, :, pl.ds(h * LANES, LANES)],
+                vin.at[span, h, pl.ds(PAD, p.ny)],
                 vsem.at[2 * c + h],
             )
             for h in range(2)
         ]
-        for c in range(CHUNKS)
+        for c, span in enumerate(spans)
     ]
     for pair in vcopies:
         for c in pair:
@@ -177,7 +188,6 @@
         return 0.5 * even + 0.25 * (odd + prev)
 
     xyz, zx, yz, zf, xf, xy, yf = sends
-    half = per // 2
     rows = p.ext[0]
     comps = []
     lane = lanes_of(8)
@@ -205,17 +215,18 @@
 
     before = None
     line = {"yz": blank, "xyz": blank}
-    for c in range(CHUNKS):
+    for c in range(len(CHUNKS)):
+        first, half = starts[c] // 2, (starts[c + 1] - starts[c]) // 2
         for copy in vcopies[c]:
             copy.wait()
         us = []
         for j in range(half):
-            i = c * half + j
+            i = first + j
             even, odd = plane_of(2 * i), plane_of(2 * i + 1)
             t = (even + even) + odd
             us.append(t if before is None else t + before)
             before = odd
-        if c == CHUNKS - 1:
+        if c == len(CHUNKS) - 1:
             us.append(before)
         count = len(us)
         if count * rows % 16:
@@ -223,7 +234,7 @@
         hi, lo = halves(jnp.concatenate(us, axis=0))
         z = dot(hi, table[...]) + dot(lo, table[...])
         for j in range(count):
-            i = c * half + j
+            i = first + j
             plane = z[j * rows : (j + 1) * rows]
             comp = plane[:, LANES:]
             comps.append(comp)
@@ -368,15 +379,15 @@
     pending = [
         pltpu.make_async_remote_copy(
             src_ref=mine,
-            dst_ref=parts.at[k + 1],
+            dst_ref=parts.at[slot],
             send_sem=asend.at[0],
             recv_sem=arecv.at[0],
             device_id=target,
             device_id_type=MESH,
         )
-        for k, target in enumerate(others)
+        for target, slot in zip(others, slots)
     ]
-    for c in reversed(pending):
+    for c in pending:
         c.start()
     parts[0] = mine[...]
     every = pltpu.make_async_remote_copy(
@@ -402,6 +413,7 @@
     lane1 = lax.broadcasted_iota(jnp.int32, (1, LANES), 1)
     outs = (o1, o2, o3, o4, o5)
     square = jnp.ones((1, 1), jnp.float32)
+    found = jnp.zeros((1, LANES), jnp.float32)
     for l in range(LEVELS):
         row = stats[0:1, :] if l == 0 else stats[1:2, :]
         if l:
@@ -410,7 +422,7 @@
         cells = devices * p.xs[l] * p.ys[l] * p.zs[l]
         mean = jnp.sum(row, axis=1, keepdims=True) * (1.0 / cells)
         before, square = square, mean + EPSILON * square
-        scales[l] = jnp.sqrt(square / before)[0, 0]
+        found = jnp.where(lane1 == l, jnp.sqrt(square / before), found)
         inverse = 1.0 / jnp.sqrt(square)
         if l == 0:
             o1[...] = grid[...] * inverse.reshape(1, 1, 1)
@@ -419,6 +431,7 @@
         block = roll(block, -p.coff[l])
         block = block.reshape(p.xs[l], p.pys[l], LANES)
         outs[l][...] = block[:, : p.ys[l], : p.zs[l]]
+    scales[...] = found[:, :LEVELS]
 
 
 def per_device(sizes, residual_in):
@@ -451,7 +464,7 @@
         + [
             pltpu.VMEM((2, LANES), f32),
             pltpu.VMEM((count, 2, LANES), f32),
-            dma((2 * CHUNKS,)),
+            dma((2 * len(CHUNKS),)),
             dma((len(HOPS),)),
             dma((len(HOPS),)),
             dma((1,)),
@@ -463,15 +476,16 @@
         name="restrict_exchange",
     )(residual_in)
     shapes = list(zip(p.xs, p.ys, p.zs))
-    return pl.pallas_call(
+    *grids, scales = pl.pallas_call(
         functools.partial(scale_kernel, p, count),
         out_shape=tuple(jax.ShapeDtypeStruct(s, f32) for s in shapes)
-        + (jax.ShapeDtypeStruct((LEVELS,), f32),),
+        + (jax.ShapeDtypeStruct((1, LEVELS), f32),),
         in_specs=[vmem] * 3,
-        out_specs=(vmem,) * 5 + (pl.BlockSpec(memory_space=pltpu.SMEM),),
+        out_specs=(vmem,) * 6,
         compiler_params=pltpu.CompilerParams(vmem_limit_bytes=8 << 20),
         name="scale_levels",
     )(grid, packed, stats)
+    return (*grids, scales.reshape(LEVELS))
 
 
 def solution(mesh):

time: 16.3 us -> 16.2 us (level)
  no operation moved by 1% of the time
where the time goes in v4:
time: 16.2 us; the launch traced here: 16 us
  Pallas kernels  15.4 us (95%)
  between operations  0.64 us (4%)
    pallas_call x1, Pallas kernels, per_device(): pl.pallas_call(functools.partial(gather_kernel, p, sizes), out_shape=(jax...  14.4 us
    pallas_call x1, Pallas kernels, per_device(): pl.pallas_call(functools.partial(scale_kernel, p, count), out_shape=tuple...  0.97 us

profile of v4, /device:TPU:0, one launch (start us, length us, event | category | flops | bytes accessed | tf_op | source)
XLA Modules:
  0.0 16.0 jit_solution(11419784176742712942)
XLA Ops:
  0.6 14.4 %restrict_exchange.1 = (f32[32,32,128]{2,1,0:T(8,128)S(1)}, f32[368,128]{1,0:T(8,128)S(1)}, f32[2,128]{1,0:T(2,128)S(1)}) custom-call(f32[64,64,256]{2,1,0:T(8,128)} %refs_0_.1), custom_call_target="tpu_custom_call" | custom-call | tf_op jit(solution)/shard_map/restrict_exchange/pallas_call | solution.py:448
  15.1 1.0 %scale_levels.1 = (f32[32,32,128]{2,1,0:T(8,128)}, f32[16,16,64]{2,1,0:T(8,128)}, f32[8,8,32]{2,1,0:T(8,128)}, f32[4,4,16]{2,1,0:T(4,128)}, f32[2,2,8]{2,1,0:T(2,128)}, /*index=5*/f32[1,5]{1,0:T(1,128)}) custom-call(f32[32,32,128]{2,1,0:T(8,128)S(1)} %get-tuple-element.15.grid, f32[368,128]{1,0:T(8,128)S(1)} %get-tuple-element.16.packed, ...), custom_call_target="tpu_custom_call" | custom-call | tf_op jit(solution)/shard_map/scale_levels/pallas_call | solution.py:479
